TPU v7x, 256 devices: a whole 4x4x8 slice. The times are simulated.
256 devices in a mesh: member: 16 (over z, y_hi), band: 16 (over y_lo, x, core).
Axes of the slice: x: 4, y: 4 (y_hi: 2, y_lo: 2; y = y_hi * 2 + y_lo), z: 8, core: 2. Of those that a mesh axis runs over, the one named last changes fastest.
Arguments:
- spectral: float32 [256, 768, 768], P('member', 'band'), parts along dimension 0, may hold values from -6 to 6
- coupling: float32 [16384, 1024], P(('member', 'band')), parts along dimension 0, may hold values from 0.02 to 162, as said below
- quadratic: float32 [16384, 1024], P(('member', 'band')), parts along dimension 0, may hold values from -1.5 to 1.5
Outputs:
- tendency_spectral: float32 [256, 768, 768], P('member', 'band'), parts along dimension 0
There are 16 independent parts, one for each index of `member`. A program takes and returns all parts, laid end to end along the dimension named above; each array names one. Nothing has to cross between parts.
Inputs may be any that keep to these rules, and one draw needn't show every extreme that they name: `coupling`: positive.
All inputs are finite; a program needn't handle non-finite values.
Results may differ from a plain program's by a relative error of at most 0.00008.
Values sent between devices are 32-bit elements; how exact they have to be, the bound alone decides.
No kernel may reach another device: no remote copies, remote signals or barrier semaphores. Data moves between devices by JAX's collectives and lax.ppermute only.
A program may use at most 128 MiB of HBM per device.

v0:
```python
import functools, math
import numpy as np
import jax
import jax.numpy as jnp
from jax import lax
from jax.experimental import pallas as pl
from jax.experimental.pallas import tpu as pltpu
from jax.sharding import Mesh
from jax.sharding import PartitionSpec as P

F32, BF16 = jnp.float32, jnp.bfloat16
LANES = 128

BAND = ("band_0", "band_1", "band_2")
MEMBER_BAND = ("member",) + BAND


def trig_table(cells, coeffs):
    half = coeffs // 2
    position = np.arange(cells)[:, None]
    column = np.arange(coeffs)[None, :]
    turns = position * (column % half) % cells
    angles = turns * (2.0 * np.pi / cells)
    return np.where(column < half, np.cos(angles), np.sin(angles)).astype(np.float32)


def split_table(table):
    high = table.astype(jnp.bfloat16)
    low = (table - high.astype(np.float32)).astype(jnp.bfloat16)
    return high, low


def split(value):
    high = value.astype(BF16)
    return high, (value - high.astype(F32)).astype(BF16)


def dot(a, b):
    return jnp.dot(a, b, preferred_element_type=F32)


def dot3(a_high, a_low, b_high, b_low):
    return dot(a_high, b_high) + dot(a_low, b_high) + dot(a_high, b_low)


def lane_halves(shape):
    return lax.broadcasted_iota(jnp.int32, shape, 1) < LANES // 2


def swap(a, b):
    left = lane_halves(a.shape)
    return (
        jnp.where(left, a, pltpu.roll(b, LANES // 2, 1)),
        jnp.where(left, pltpu.roll(a, LANES // 2, 1), b),
    )


def synth_y(levels, rows, bands, x_ref, th_ref, tl_ref, o_ref, xh, xl, acc):
    m = levels * rows
    high, low = split(x_ref[...].reshape(m, x_ref.shape[2]))
    xh[...] = high
    xl[...] = low

    @pl.loop(0, th_ref.shape[1] // 256)
    def _(j):
        cols = pl.ds(pl.multiple_of(j * 256, 256), 256)
        acc[...] = dot3(xh[...], xl[...], th_ref[:, cols], tl_ref[:, cols])
        for p in range(levels // 2):
            for h in range(2):
                a = acc[2 * p * rows : (2 * p + 1) * rows, h * LANES : (h + 1) * LANES]
                b = acc[(2 * p + 1) * rows : (2 * p + 2) * rows, h * LANES : (h + 1) * LANES]
                even, odd = swap(a, b)
                o_ref[4 * j + 2 * h, :, p * LANES : (p + 1) * LANES] = even
                o_ref[4 * j + 2 * h + 1, :, p * LANES : (p + 1) * LANES] = odd


def synth_x(r_ref, th_ref, tl_ref, c_ref, p_ref, e_ref, rh, rl):
    k = rh.shape[0]
    n = rh.shape[1]
    high, low = split(r_ref[...].reshape(k, n))
    rh[...] = high
    rl[...] = low
    e_ref[...] = jnp.zeros_like(e_ref)

    for j in range(n // 256):
        cols = slice(j * 256, (j + 1) * 256)
        p_ref[:, cols] = dot3(th_ref[...], tl_ref[...], rh[:, cols], rl[:, cols])
        for h in range(2):
            lanes = slice(j * 256 + h * LANES, j * 256 + (h + 1) * LANES)
            product = p_ref[:, lanes] * c_ref[...]
            p_ref[:, lanes] = product
            total = jnp.sum(product * product, axis=0, keepdims=True)
            for d in range(e_ref.shape[0]):
                e_ref[d, 2 * j + h : 2 * j + h + 1, :] = total


def group_sum(v):
    lane = lax.broadcasted_iota(jnp.int32, v.shape, 1)
    step = 1
    while step < LANES // 2:
        v = v + jnp.where(lane % (2 * step) < step, pltpu.roll(v, LANES - step, 1), pltpu.roll(v, step, 1))
        step *= 2
    return v


def analyse_x(points, p_ref, e_ref, q_ref, th_ref, tl_ref, o_ref, gh, gl, acc):
    m = acc.shape[0]
    n = p_ref.shape[1]
    rows = o_ref.shape[1]
    total = group_sum(jnp.sum(e_ref[...], axis=0))
    scale = lax.rsqrt(total * (1.0 / points) + 1e-06)
    half = m // 2
    row = lax.broadcasted_iota(jnp.int32, (m, 1), 0)
    weight = jnp.where(row % half == 0, 1.0, 2.0).astype(F32)
    for t in range(n // LANES):
        lanes = slice(t * LANES, (t + 1) * LANES)
        scaled = p_ref[:, lanes] * scale[t : t + 1, :]
        high, low = split(scaled + q_ref[...] * scaled * scaled)
        gh[:, lanes] = high
        gl[:, lanes] = low
    for j in range(n // 256):
        cols = slice(j * 256, (j + 1) * 256)
        value = dot3(th_ref[...], tl_ref[...], gh[:, cols], gl[:, cols]) * weight
        o_ref[:, :, cols] = value.reshape(m // rows, rows, 256)


def analyse_y(levels, factor, r_ref, th_ref, tl_ref, o_ref, yh, yl):
    bands, rows = r_ref.shape[0], r_ref.shape[1]
    for p in range(levels // 2):
        for s in range(bands // 2):
            a = r_ref[2 * s, :, p * LANES : (p + 1) * LANES]
            b = r_ref[2 * s + 1, :, p * LANES : (p + 1) * LANES]
            for i, piece in enumerate(swap(a, b)):
                high, low = split(piece)
                at = (2 * p + i) * rows
                yh[at : at + rows, s * LANES : (s + 1) * LANES] = high
                yl[at : at + rows, s * LANES : (s + 1) * LANES] = low
    coeffs = th_ref.shape[1]
    for j in range(coeffs // 256):
        cols = slice(j * 256, (j + 1) * 256)
        col = j * 256 + lax.broadcasted_iota(jnp.int32, (1, 256), 1)
        weight = jnp.where(col % (coeffs // 2) == 0, factor, 2.0 * factor).astype(F32)
        value = dot3(yh[...], yl[...], th_ref[:, cols], tl_ref[:, cols]) * weight
        o_ref[:, :, cols] = value.reshape(levels, rows, 256)


CHUNKS = 1


def stage(kernel, out_shape, scratch, flops, nbytes):
    return pl.pallas_call(
        kernel,
        out_shape=out_shape,
        scratch_shapes=scratch,
        compiler_params=pltpu.CompilerParams(vmem_limit_bytes=40 * 1024 * 1024),
        cost_estimate=pl.CostEstimate(flops=flops, bytes_accessed=nbytes, transcendentals=0),
    )


def on_device(bands, spectral, coupling, quadratic):
    levels, rows, coeffs = spectral.shape
    own, cells = coupling.shape
    table = trig_table(cells, coeffs)
    th, tl = (jnp.asarray(t) for t in split_table(table))
    uh, ul = (jnp.asarray(t) for t in split_table(np.ascontiguousarray(table.T)))
    count = levels // CHUNKS
    n = count * own
    flops = 6 * count * own * cells * coeffs
    nbytes = 4 * n * (cells + coeffs) + 4 * cells * coeffs
    ct = coupling.T * (1.0 / (coeffs // 2))
    ct = jnp.concatenate([ct, ct], axis=1)
    qt = jnp.concatenate([quadratic.T, quadratic.T], axis=1)
    factor = (coeffs // 2) / float(cells * cells)
    spread = jax.ShapeDtypeStruct((bands, rows, n), F32)

    def exchange(a):
        return lax.all_to_all(a, BAND, 0, 0, tiled=True)

    first = stage(
        functools.partial(synth_y, count, rows, bands),
        spread,
        [pltpu.VMEM((count * rows, coeffs), BF16)] * 2 + [pltpu.VMEM((count * rows, 256), F32)],
        flops, nbytes,
    )
    second = stage(
        synth_x,
        (jax.ShapeDtypeStruct((cells, n), F32), jax.ShapeDtypeStruct((bands, 8, LANES), F32)),
        [pltpu.VMEM((coeffs, n), BF16)] * 2,
        flops, nbytes,
    )
    third = stage(
        functools.partial(analyse_x, float(cells * cells)),
        spread,
        [pltpu.VMEM((cells, n), BF16)] * 2 + [pltpu.VMEM((coeffs, 256), F32)],
        flops, nbytes,
    )
    fourth = stage(
        functools.partial(analyse_y, count, factor),
        jax.ShapeDtypeStruct((count, rows, coeffs), F32),
        [pltpu.VMEM((count * rows, cells), BF16)] * 2,
        flops, nbytes,
    )
    done = []
    for k in range(CHUNKS):
        sent = first(spectral[k * count : (k + 1) * count], uh, ul)
        turned = exchange(sent)
        product, energy = second(turned, th, tl, ct)
        energy = exchange(energy)
        back = third(product, energy, qt, uh, ul)
        done.append(fourth(exchange(back), th, tl))
    return jnp.concatenate(done, axis=0) if CHUNKS > 1 else done[0]


def solution(mesh):
    torus = Mesh(
        mesh.devices.reshape(mesh.shape["member"], 2, 4, 2),
        ("member",) + BAND,
    )
    return jax.shard_map(
        functools.partial(on_device, mesh.shape["band"]),
        mesh=torus,
        in_specs=(P("member", BAND, None), P(MEMBER_BAND, None), P(MEMBER_BAND, None)),
        out_specs=P("member", BAND, None),
        check_vma=False,
    )
```

profile of v0, /device:TPU:1, one launch (start us, length us, event | category | flops | bytes accessed | tf_op | source)
XLA Modules:
  0.0 139.3 jit_solution(4223715904820200131)
XLA Ops:
  0.0 0.0 copy-start.2
  0.0 1.7 %copy-done.2 = f32[16,48,768]{2,1,0:T(8,128)S(1)} copy-done((f32[16,48,768]{2,1,0:T(8,128)S(1)}, f32[16,48,768]{2,1,0:T(8,128)}, u32[]{:S(2)}) %copy-start.2) | copy-done | bytes 2359320
  1.7 0.0 copy-start.7
  1.7 1.4 %copy-done.7 = bf16[768,1024]{1,0:T(8,128)(2,1)S(1)} copy-done((bf16[768,1024]{1,0:T(8,128)(2,1)S(1)}, bf16[768,1024]{1,0:T(8,128)(2,1)}, u32[]{:S(2)}) %copy-start.7) | copy-done | bytes 1572888
  3.1 0.0 copy-start.9
  3.1 1.4 %copy-done.9 = bf16[768,1024]{1,0:T(8,128)(2,1)S(1)} copy-done((bf16[768,1024]{1,0:T(8,128)(2,1)S(1)}, bf16[768,1024]{1,0:T(8,128)(2,1)}, u32[]{:S(2)}) %copy-start.9) | copy-done | bytes 1572888
  4.5 5.0 %shard_map.73 = f32[16,48,1024]{2,1,0:T(8,128)S(1)} custom-call(f32[16,48,768]{2,1,0:T(8,128)S(1)} %copy-done.2, bf16[768,1024]{1,0:T(8,128)(2,1)S(1)} %copy-done.7, bf16[768,1024]{1,0:T(8,128)(2,1)S(1)} %copy-done.9), custom_call_target="tpu_custom_call" | custom-call | flops 4831838208 | bytes 10485760 | tf_op jit(solution)/shard_map/pallas_call | solution.py:205
  9.5 0.0 copy-start
  9.5 1.6 %copy-done = f32[16,48,1024]{2,1,0:T(8,128)} copy-done((f32[16,48,1024]{2,1,0:T(8,128)}, f32[16,48,1024]{2,1,0:T(8,128)S(1)}, u32[]{:S(2)}) %copy-start) | copy-done | bytes 3145752
  11.1 0.0 copy-start.13
  11.1 6.9 %all-to-all-start = ((f32[16,48,1024]{2,1,0:T(8,128)}), f32[16,48,1024]{2,1,0:T(8,128)S(1)}, u32[]{:S(2)}, u32[]{:S(2)}) async-start(f32[16,48,1024]{2,1,0:T(8,128)} %copy-done), calls=%async_computation | async-start | bytes 6291456 | tf_op jit(solution)/shard_map/all_to_all | solution.py:177
  18.1 0.0 copy-done.13
  18.1 1.0 copy.10
  19.1 2.0 %copy.12 = f32[64,1024]{0,1:T(8,128)} copy(f32[64,1024]{1,0:T(8,128)} %param.9) | data formatting | bytes 524288 | tf_op args[2]
  21.0 1.1 multiply_bitcast_fusion
  22.1 1.0 pad_maximum_fusion.c_ref
  23.1 36.8 %all-to-all-done.r_ref = f32[16,48,1024]{2,1,0:T(8,128)S(1)} async-done(((f32[16,48,1024]{2,1,0:T(8,128)}), f32[16,48,1024]{2,1,0:T(8,128)S(1)}, u32[]{:S(2)}, u32[]{:S(2)}) %all-to-all-start) | async-done | bytes 3145760 | tf_op jit(solution)/shard_map/all_to_all | solution.py:177
  59.9 0.0 copy-start.1
  59.9 1.0 copy-done.1
  60.9 0.0 copy-start.3
  60.9 1.4 %copy-done.3 = bf16[1024,768]{1,0:T(8,128)(2,1)S(1)} copy-done((bf16[1024,768]{1,0:T(8,128)(2,1)S(1)}, bf16[1024,768]{1,0:T(8,128)(2,1)}, u32[]{:S(2)}) %copy-start.3) | copy-done | bytes 1572888
  62.3 0.0 copy-start.5
  62.4 1.4 %copy-done.5 = bf16[1024,768]{1,0:T(8,128)(2,1)S(1)} copy-done((bf16[1024,768]{1,0:T(8,128)(2,1)S(1)}, bf16[1024,768]{1,0:T(8,128)(2,1)}, u32[]{:S(2)}) %copy-start.5) | copy-done | bytes 1572888
  63.8 5.7 %shard_map.74 = (f32[1024,1024]{1,0:T(8,128)S(1)}, f32[16,8,128]{2,1,0:T(8,128)}) custom-call(f32[16,48,1024]{2,1,0:T(8,128)S(1)} %all-to-all-done.r_ref, bf16[1024,768]{1,0:T(8,128)(2,1)S(1)} %copy-done.3, bf16[1024,768]{1,0:T(8,128)(2,1)S(1)} %copy-done.5, f32[1024,128]{1,0:T(8,128)S(1)} %copy-done.1), custom_call_target="tpu_custom_call" | custom-call | flops 4831838208 | bytes 10485760 | tf_op jit(solution)/shard_map/pallas_call | solution.py:207
  69.4 0.0 copy-start.11
  69.4 2.0 %copy-done.11 = f32[1024,1024]{1,0:T(8,128)} copy-done((f32[1024,1024]{1,0:T(8,128)}, f32[1024,1024]{1,0:T(8,128)S(1)}, u32[]{:S(2)}) %copy-start.11) | copy-done | bytes 4194328
  71.4 4.6 %all-to-all-start.1 = ((f32[16,8,128]{2,1,0:T(8,128)}), f32[16,8,128]{2,1,0:T(8,128)S(1)}, u32[]{:S(2)}, u32[]{:S(2)}) async-start(f32[16,8,128]{2,1,0:T(8,128)} %get-tuple-element.8), calls=%async_computation.1 | async-start | bytes 131072 | tf_op jit(solution)/shard_map/all_to_all | solution.py:177
  76.0 1.4 %pad_maximum_fusion.1.q_ref = f32[1024,128]{1,0:T(8,128)S(1)} fusion(f32[1024,64]{1,0:T(8,128)} %bitcast.3), kind=kLoop, calls=%fused_computation.1 | loop fusion | flops 131072 | bytes 786432 | tf_op jit(solution)/shard_map/concatenate | solution.py:172
  77.4 4.4 %all-to-all-done.1.e_ref = f32[16,8,128]{2,1,0:T(8,128)S(1)} async-done(((f32[16,8,128]{2,1,0:T(8,128)}), f32[16,8,128]{2,1,0:T(8,128)S(1)}, u32[]{:S(2)}, u32[]{:S(2)}) %all-to-all-start.1) | async-done | bytes 65568 | tf_op jit(solution)/shard_map/all_to_all | solution.py:177
  81.8 0.0 copy-start.8
  81.8 1.4 %copy-done.8 = bf16[768,1024]{1,0:T(8,128)(2,1)S(1)} copy-done((bf16[768,1024]{1,0:T(8,128)(2,1)S(1)}, bf16[768,1024]{1,0:T(8,128)(2,1)}, u32[]{:S(2)}) %copy-start.8) | copy-done | bytes 1572888
  83.2 0.0 copy-start.10
  83.2 1.4 %copy-done.10 = bf16[768,1024]{1,0:T(8,128)(2,1)S(1)} copy-done((bf16[768,1024]{1,0:T(8,128)(2,1)S(1)}, bf16[768,1024]{1,0:T(8,128)(2,1)}, u32[]{:S(2)}) %copy-start.10) | copy-done | bytes 1572888
  84.6 0.0 copy-start.12
  84.6 2.2 %copy-done.12 = f32[1024,1024]{1,0:T(8,128)S(1)} copy-done((f32[1024,1024]{1,0:T(8,128)S(1)}, f32[1024,1024]{1,0:T(8,128)}, u32[]{:S(2)}) %copy-start.12) | copy-done | bytes 4194328
  86.8 5.8 %shard_map.75 = f32[16,48,1024]{2,1,0:T(8,128)S(1)} custom-call(f32[1024,1024]{1,0:T(8,128)S(1)} %copy-done.12, f32[16,8,128]{2,1,0:T(8,128)S(1)} %all-to-all-done.1.e_ref, f32[1024,128]{1,0:T(8,128)S(1)} %pad_maximum_fusion.1.q_ref, bf16[768,1024]{1,0:T(8,128)(2,1)S(1)} %copy-done.8, bf16[768,1024]{1,0:T(8,128)(2,1)S(1)} %copy-done.10), custom_call_target="tpu_custom_call" | custom-call | flops 4831838208 | bytes 10485760 | tf_op jit(solution)/shard_map/pallas_call | solution.py:209
  92.6 0.0 copy-start.4
  92.6 0.0 copy-start.6
  92.7 40.8 %all_to_all.15.r_ref = f32[16,48,1024]{2,1,0:T(8,128)S(1)} all-to-all(f32[16,48,1024]{2,1,0:T(8,128)S(1)} %shard_map.75), channel_id=1, replica_groups=mesh['member'=16,'band_0'=2,'band_1'=4,'band_2'=2] {'band_0','band_1','b..., dimensions={0} | all-to-all | bytes 6291456 | tf_op jit(solution)/shard_map/all_to_all | solution.py:177
  133.5 0.0 copy-done.4
  133.5 0.0 copy-done.6
  133.5 5.8 %shard_map.76 = f32[16,48,768]{2,1,0:T(8,128)} custom-call(f32[16,48,1024]{2,1,0:T(8,128)S(1)} %all_to_all.15.r_ref, bf16[1024,768]{1,0:T(8,128)(2,1)S(1)} %copy-done.4, bf16[1024,768]{1,0:T(8,128)(2,1)S(1)} %copy-done.6), custom_call_target="tpu_custom_call" | custom-call | flops 4831838208 | bytes 10485760 | tf_op jit(solution)/shard_map/pallas_call | solution.py:210
Async XLA Ops:
  0.0 1.7 %copy-start.2 = (f32[16,48,768]{2,1,0:T(8,128)S(1)}, f32[16,48,768]{2,1,0:T(8,128)}, u32[]{:S(2)}) copy-start(f32[16,48,768]{2,1,0:T(8,128)} %x_ref.1) | copy-start | bytes 7077892
  1.7 1.4 %copy-start.7 = (bf16[768,1024]{1,0:T(8,128)(2,1)S(1)}, bf16[768,1024]{1,0:T(8,128)(2,1)}, u32[]{:S(2)}) copy-start(bf16[768,1024]{1,0:T(8,128)(2,1)} %constant.12.clone.th_ref) | copy-start | bytes 4718596
  3.1 1.4 %copy-start.9 = (bf16[768,1024]{1,0:T(8,128)(2,1)S(1)}, bf16[768,1024]{1,0:T(8,128)(2,1)}, u32[]{:S(2)}) copy-start(bf16[768,1024]{1,0:T(8,128)(2,1)} %constant.13.clone.tl_ref) | copy-start | bytes 4718596
  9.5 1.6 %copy-start = (f32[16,48,1024]{2,1,0:T(8,128)}, f32[16,48,1024]{2,1,0:T(8,128)S(1)}, u32[]{:S(2)}) copy-start(f32[16,48,1024]{2,1,0:T(8,128)S(1)} %shard_map.73) | copy-start | bytes 9437188
  11.1 6.9 %copy-start.13 = (f32[64,1024]{1,0:T(8,128)S(1)}, f32[64,1024]{1,0:T(8,128)}, u32[]{:S(2)}) copy-start(f32[64,1024]{1,0:T(8,128)} %param.8) | copy-start | bytes 786436
  11.1 48.8 %all-to-all-start = ((f32[16,48,1024]{2,1,0:T(8,128)}), f32[16,48,1024]{2,1,0:T(8,128)S(1)}, u32[]{:S(2)}, u32[]{:S(2)}) async-start(f32[16,48,1024]{2,1,0:T(8,128)} %copy-done), calls=%async_computation | async-start | bytes 6291456 | tf_op jit(solution)/shard_map/all_to_all | solution.py:177
  59.9 1.0 copy-start.1
  60.9 1.4 %copy-start.3 = (bf16[1024,768]{1,0:T(8,128)(2,1)S(1)}, bf16[1024,768]{1,0:T(8,128)(2,1)}, u32[]{:S(2)}) copy-start(bf16[1024,768]{1,0:T(8,128)(2,1)} %constant.10.clone.th_ref) | copy-start | bytes 4718596
  62.3 1.4 %copy-start.5 = (bf16[1024,768]{1,0:T(8,128)(2,1)S(1)}, bf16[1024,768]{1,0:T(8,128)(2,1)}, u32[]{:S(2)}) copy-start(bf16[1024,768]{1,0:T(8,128)(2,1)} %constant.11.clone.tl_ref) | copy-start | bytes 4718596
  69.4 2.0 %copy-start.11 = (f32[1024,1024]{1,0:T(8,128)}, f32[1024,1024]{1,0:T(8,128)S(1)}, u32[]{:S(2)}) copy-start(f32[1024,1024]{1,0:T(8,128)S(1)} %get-tuple-element.7.p_ref) | copy-start | bytes 12582916
  71.4 10.4 %all-to-all-start.1 = ((f32[16,8,128]{2,1,0:T(8,128)}), f32[16,8,128]{2,1,0:T(8,128)S(1)}, u32[]{:S(2)}, u32[]{:S(2)}) async-start(f32[16,8,128]{2,1,0:T(8,128)} %get-tuple-element.8), calls=%async_computation.1 | async-start | bytes 131072 | tf_op jit(solution)/shard_map/all_to_all | solution.py:177
  81.8 1.4 %copy-start.8 = (bf16[768,1024]{1,0:T(8,128)(2,1)S(1)}, bf16[768,1024]{1,0:T(8,128)(2,1)}, u32[]{:S(2)}) copy-start(bf16[768,1024]{1,0:T(8,128)(2,1)} %constant.12.clone.th_ref) | copy-start | bytes 4718596
  83.2 1.4 %copy-start.10 = (bf16[768,1024]{1,0:T(8,128)(2,1)S(1)}, bf16[768,1024]{1,0:T(8,128)(2,1)}, u32[]{:S(2)}) copy-start(bf16[768,1024]{1,0:T(8,128)(2,1)} %constant.13.clone.tl_ref) | copy-start | bytes 4718596
  84.6 2.2 %copy-start.12 = (f32[1024,1024]{1,0:T(8,128)S(1)}, f32[1024,1024]{1,0:T(8,128)}, u32[]{:S(2)}) copy-start(f32[1024,1024]{1,0:T(8,128)} %copy-done.11) | copy-start | bytes 12582916
  92.6 40.8 %copy-start.4 = (bf16[1024,768]{1,0:T(8,128)(2,1)S(1)}, bf16[1024,768]{1,0:T(8,128)(2,1)}, u32[]{:S(2)}) copy-start(bf16[1024,768]{1,0:T(8,128)(2,1)} %constant.10.clone.th_ref) | copy-start | bytes 4718596
  92.6 40.8 %copy-start.6 = (bf16[1024,768]{1,0:T(8,128)(2,1)S(1)}, bf16[1024,768]{1,0:T(8,128)(2,1)}, u32[]{:S(2)}) copy-start(bf16[1024,768]{1,0:T(8,128)(2,1)} %constant.11.clone.tl_ref) | copy-start | bytes 4718596
where the time goes:
time: 140 us; the launch traced here: 139 us
  waiting for transfers between devices  41.2 us (29%)
  blocking collectives  40.8 us (29%)
  Pallas kernels  22.3 us (16%)
  local copies, waits for them, and re-layouts  19.9 us (14%)
  starting transfers between devices  11.5 us (8%)
  other arithmetic  3.49 us (2%)
    all_to_all x2, waiting for transfers between devices, exchange(): return lax.all_to_all(a, BAND, 0, 0, tiled=True)  41.2 us
    all_to_all x1, blocking collectives, exchange(): return lax.all_to_all(a, BAND, 0, 0, tiled=True)  40.8 us
    unnamed x30, local copies, waits for them, and re-layouts  19.9 us
    all_to_all x2, starting transfers between devices, exchange(): return lax.all_to_all(a, BAND, 0, 0, tiled=True)  11.5 us
    pallas_call x1, Pallas kernels, on_device(): done.append(fourth(exchange(back), th, tl))  5.82 us
    pallas_call x1, Pallas kernels, on_device(): back = third(product, energy, qt, uh, ul)  5.8 us
    pallas_call x1, Pallas kernels, on_device(): product, energy = second(turned, th, tl, ct)  5.68 us
    pallas_call x1, Pallas kernels, on_device(): sent = first(spectral[k * count:(k + 1) * count], uh, ul)  4.98 us
  transfers between devices with their start and end apart: 2, of which 2 were waited for; matrix products, arithmetic and copies ran while one was open for 5% of the time, Pallas kernels for 0%

commit v1 on v0

--- a/solution.py
+++ b/solution.py
@@ -74,9 +74,14 @@
                 o_ref[4 * j + 2 * h + 1, :, p * LANES : (p + 1) * LANES] = odd
 
 
+def doubled_columns(a):
+    return jnp.concatenate([a, a], axis=0).T
+
+
 def synth_x(r_ref, th_ref, tl_ref, c_ref, p_ref, e_ref, rh, rl):
     k = rh.shape[0]
     n = rh.shape[1]
+    coupling = doubled_columns(c_ref[...]) * (1.0 / (k // 2))
     high, low = split(r_ref[...].reshape(k, n))
     rh[...] = high
     rl[...] = low
@@ -87,7 +92,7 @@
         p_ref[:, cols] = dot3(th_ref[...], tl_ref[...], rh[:, cols], rl[:, cols])
         for h in range(2):
             lanes = slice(j * 256 + h * LANES, j * 256 + (h + 1) * LANES)
-            product = p_ref[:, lanes] * c_ref[...]
+            product = p_ref[:, lanes] * coupling
             p_ref[:, lanes] = product
             total = jnp.sum(product * product, axis=0, keepdims=True)
             for d in range(e_ref.shape[0]):
@@ -107,6 +112,7 @@
     m = acc.shape[0]
     n = p_ref.shape[1]
     rows = o_ref.shape[1]
+    quadratic = doubled_columns(q_ref[...])
     total = group_sum(jnp.sum(e_ref[...], axis=0))
     scale = lax.rsqrt(total * (1.0 / points) + 1e-06)
     half = m // 2
@@ -115,7 +121,7 @@
     for t in range(n // LANES):
         lanes = slice(t * LANES, (t + 1) * LANES)
         scaled = p_ref[:, lanes] * scale[t : t + 1, :]
-        high, low = split(scaled + q_ref[...] * scaled * scaled)
+        high, low = split(scaled + quadratic * scaled * scaled)
         gh[:, lanes] = high
         gl[:, lanes] = low
     for j in range(n // 256):
@@ -152,7 +158,7 @@
         kernel,
         out_shape=out_shape,
         scratch_shapes=scratch,
-        compiler_params=pltpu.CompilerParams(vmem_limit_bytes=40 * 1024 * 1024),
+        compiler_params=pltpu.CompilerParams(vmem_limit_bytes=16 * 1024 * 1024),
         cost_estimate=pl.CostEstimate(flops=flops, bytes_accessed=nbytes, transcendentals=0),
     )
 
@@ -167,9 +173,6 @@
     n = count * own
     flops = 6 * count * own * cells * coeffs
     nbytes = 4 * n * (cells + coeffs) + 4 * cells * coeffs
-    ct = coupling.T * (1.0 / (coeffs // 2))
-    ct = jnp.concatenate([ct, ct], axis=1)
-    qt = jnp.concatenate([quadratic.T, quadratic.T], axis=1)
     factor = (coeffs // 2) / float(cells * cells)
     spread = jax.ShapeDtypeStruct((bands, rows, n), F32)
 
@@ -204,9 +207,9 @@
     for k in range(CHUNKS):
         sent = first(spectral[k * count : (k + 1) * count], uh, ul)
         turned = exchange(sent)
-        product, energy = second(turned, th, tl, ct)
+        product, energy = second(turned, th, tl, coupling)
         energy = exchange(energy)
-        back = third(product, energy, qt, uh, ul)
+        back = third(product, energy, quadratic, uh, ul)
         done.append(fourth(exchange(back), th, tl))
     return jnp.concatenate(done, axis=0) if CHUNKS > 1 else done[0]
 

time: 140 us -> 122 us (0.87)
  blocking collectives: 40.8 us -> 94.7 us
  waiting for transfers between devices: 41.2 us -> 0 us
  local copies, waits for them, and re-layouts: 19.9 us -> 4.52 us
  starting transfers between devices: 11.5 us -> 0 us
  other arithmetic: 3.49 us -> 0 us
    all_to_all x1 -> x3, blocking collectives: 40.8 us -> 94.7 us  [exchange(): return lax.all_to_all(a, BAND, 0, 0, tiled=True)]
    all_to_all x2 -> x0, waiting for transfers between devices: 41.2 us -> none  [exchange(): return lax.all_to_all(a, BAND, 0, 0, tiled=True)]
    unnamed x30 -> x18, local copies, waits for them, and re-layouts: 19.9 us -> 4.52 us
    all_to_all x2 -> x0, starting transfers between devices: 11.5 us -> none  [exchange(): return lax.all_to_all(a, BAND, 0, 0, tiled=True)]
    concatenate x2 -> x0, other arithmetic: 2.4 us -> none  [the longest x1 1.4 us: on_device(): qt = jnp.concatenate([quadratic.T, quadratic.T], axis=1)]
  transfers between devices with their start and end apart: 2 -> 0, of which waited for: 2 -> 0; matrix products, arithmetic and copies ran while one was open for 5% -> 0% of each run, Pallas kernels for 0% -> 0%
where the time goes in v1:
time: 122 us
  blocking collectives  94.7 us (78%)
  Pallas kernels  22.5 us (18%)
  local copies, waits for them, and re-layouts  4.52 us (4%)
    all_to_all x3, blocking collectives, exchange(): return lax.all_to_all(a, BAND, 0, 0, tiled=True)  94.7 us
    pallas_call x1, Pallas kernels, on_device(): back = third(product, energy, quadratic, uh, ul)  6.64 us
    pallas_call x1, Pallas kernels, on_device(): done.append(fourth(exchange(back), th, tl))  5.82 us
    pallas_call x1, Pallas kernels, on_device(): product, energy = second(turned, th, tl, coupling)  5.09 us
    pallas_call x1, Pallas kernels, on_device(): sent = first(spectral[k * count:(k + 1) * count], uh, ul)  4.98 us
    unnamed x18, local copies, waits for them, and re-layouts  4.52 us

profile of v1, /device:TPU:1, one launch (start us, length us, event | category | flops | bytes accessed | tf_op | source)
XLA Modules:
  0.0 121.9 jit_solution(2554438475099003043)
XLA Ops:
  0.0 0.0 copy-start
  0.0 1.7 %copy-done = f32[16,48,768]{2,1,0:T(8,128)S(1)} copy-done((f32[16,48,768]{2,1,0:T(8,128)S(1)}, f32[16,48,768]{2,1,0:T(8,128)}, u32[]{:S(2)}) %copy-start) | copy-done | bytes 2359320
  1.7 0.0 copy-start.5
  1.7 1.4 %copy-done.5 = bf16[768,1024]{1,0:T(8,128)(2,1)S(1)} copy-done((bf16[768,1024]{1,0:T(8,128)(2,1)S(1)}, bf16[768,1024]{1,0:T(8,128)(2,1)}, u32[]{:S(2)}) %copy-start.5) | copy-done | bytes 1572888
  3.1 0.0 copy-start.7
  3.1 1.4 %copy-done.7 = bf16[768,1024]{1,0:T(8,128)(2,1)S(1)} copy-done((bf16[768,1024]{1,0:T(8,128)(2,1)S(1)}, bf16[768,1024]{1,0:T(8,128)(2,1)}, u32[]{:S(2)}) %copy-start.7) | copy-done | bytes 1572888
  4.5 5.0 %shard_map.73 = f32[16,48,1024]{2,1,0:T(8,128)S(1)} custom-call(f32[16,48,768]{2,1,0:T(8,128)S(1)} %copy-done, bf16[768,1024]{1,0:T(8,128)(2,1)S(1)} %copy-done.7, bf16[768,1024]{1,0:T(8,128)(2,1)S(1)} %copy-done.5), custom_call_target="tpu_custom_call" | custom-call | flops 4831838208 | bytes 10485760 | tf_op jit(solution)/shard_map/pallas_call | solution.py:208
  9.5 0.0 copy-start.1
  9.5 0.0 copy-start.3
  9.5 0.0 copy-start.4
  9.5 44.5 %all_to_all.15.r_ref = f32[16,48,1024]{2,1,0:T(8,128)S(1)} all-to-all(f32[16,48,1024]{2,1,0:T(8,128)S(1)} %shard_map.73), channel_id=1, replica_groups=mesh['member'=16,'band_0'=2,'band_1'=4,'band_2'=2] {'band_0','band_1','b..., dimensions={0} | all-to-all | bytes 6291456 | tf_op jit(solution)/shard_map/all_to_all | solution.py:180
  54.0 0.0 copy-done.1
  54.0 0.0 copy-done.3
  54.0 0.0 copy-done.4
  54.0 0.0 copy-start.2
  54.0 0.0 copy-start.6
  54.0 0.0 copy-start.8
  54.0 5.1 %shard_map.74 = (f32[1024,1024]{1,0:T(8,128)S(1)}, f32[16,8,128]{2,1,0:T(8,128)S(1)}) custom-call(f32[16,48,1024]{2,1,0:T(8,128)S(1)} %all_to_all.15.r_ref, bf16[1024,768]{1,0:T(8,128)(2,1)S(1)} %copy-done.4, bf16[1024,768]{1,0:T(8,128)(2,1)S(1)} %copy-done.3, f32[64,1024]{1,0:T(8,128)S(1)} %copy-done.1), custom_call_target="tpu_custom_call" | custom-call | flops 4831838208 | bytes 10485760 | tf_op jit(solution)/shard_map/pallas_call | solution.py:210
  59.1 9.7 %all_to_all.16.e_ref = f32[16,8,128]{2,1,0:T(8,128)S(1)} all-to-all(f32[16,8,128]{2,1,0:T(8,128)S(1)} %get-tuple-element.8), channel_id=1, replica_groups=mesh['member'=16,'band_0'=2,'band_1'=4,'band_2'=2] {'band_0','band_1','b..., dimensions={0} | all-to-all | bytes 131072 | tf_op jit(solution)/shard_map/all_to_all | solution.py:180
  68.8 0.0 copy-done.2
  68.8 0.0 copy-done.6
  68.8 0.0 copy-done.8
  68.8 6.6 %shard_map.75 = f32[16,48,1024]{2,1,0:T(8,128)S(1)} custom-call(f32[1024,1024]{1,0:T(8,128)S(1)} %get-tuple-element.7.p_ref, f32[16,8,128]{2,1,0:T(8,128)S(1)} %all_to_all.16.e_ref, f32[64,1024]{1,0:T(8,128)S(1)} %copy-done.2, bf16[768,1024]{1,0:T(8,128)(2,1)S(1)} %copy-done.8, bf16[768,1024]{1,0:T(8,128)(2,1)S(1)} %copy-done.6), custom_call_target="tpu_custom_call" | custom-call | flops 4831838208 | bytes 10485760 | tf_op jit(solution)/shard_map/pallas_call | solution.py:212
  75.5 40.5 %all_to_all.17.r_ref = f32[16,48,1024]{2,1,0:T(8,128)S(1)} all-to-all(f32[16,48,1024]{2,1,0:T(8,128)S(1)} %shard_map.75), channel_id=1, replica_groups=mesh['member'=16,'band_0'=2,'band_1'=4,'band_2'=2] {'band_0','band_1','b..., dimensions={0} | all-to-all | bytes 6291456 | tf_op jit(solution)/shard_map/all_to_all | solution.py:180
  116.0 5.8 %shard_map.76 = f32[16,48,768]{2,1,0:T(8,128)} custom-call(f32[16,48,1024]{2,1,0:T(8,128)S(1)} %all_to_all.17.r_ref, bf16[1024,768]{1,0:T(8,128)(2,1)S(1)} %copy-done.4, bf16[1024,768]{1,0:T(8,128)(2,1)S(1)} %copy-done.3), custom_call_target="tpu_custom_call" | custom-call | flops 4831838208 | bytes 10485760 | tf_op jit(solution)/shard_map/pallas_call | solution.py:213
Async XLA Ops:
  0.0 1.7 %copy-start = (f32[16,48,768]{2,1,0:T(8,128)S(1)}, f32[16,48,768]{2,1,0:T(8,128)}, u32[]{:S(2)}) copy-start(f32[16,48,768]{2,1,0:T(8,128)} %x_ref.1) | copy-start | bytes 7077892
  1.7 1.4 %copy-start.5 = (bf16[768,1024]{1,0:T(8,128)(2,1)S(1)}, bf16[768,1024]{1,0:T(8,128)(2,1)}, u32[]{:S(2)}) copy-start(bf16[768,1024]{1,0:T(8,128)(2,1)} %constant.11.clone.tl_ref) | copy-start | bytes 4718596
  3.1 1.4 %copy-start.7 = (bf16[768,1024]{1,0:T(8,128)(2,1)S(1)}, bf16[768,1024]{1,0:T(8,128)(2,1)}, u32[]{:S(2)}) copy-start(bf16[768,1024]{1,0:T(8,128)(2,1)} %constant.10.clone.th_ref) | copy-start | bytes 4718596
  9.5 44.5 %copy-start.1 = (f32[64,1024]{1,0:T(8,128)S(1)}, f32[64,1024]{1,0:T(8,128)}, u32[]{:S(2)}) copy-start(f32[64,1024]{1,0:T(8,128)} %c_ref.1) | copy-start | bytes 786436
  9.5 44.5 %copy-start.3 = (bf16[1024,768]{1,0:T(8,128)(2,1)S(1)}, bf16[1024,768]{1,0:T(8,128)(2,1)}, u32[]{:S(2)}) copy-start(bf16[1024,768]{1,0:T(8,128)(2,1)} %constant.9.clone.tl_ref) | copy-start | bytes 4718596
  9.5 44.5 %copy-start.4 = (bf16[1024,768]{1,0:T(8,128)(2,1)S(1)}, bf16[1024,768]{1,0:T(8,128)(2,1)}, u32[]{:S(2)}) copy-start(bf16[1024,768]{1,0:T(8,128)(2,1)} %constant.8.clone.th_ref) | copy-start | bytes 4718596
  54.0 14.9 %copy-start.2 = (f32[64,1024]{1,0:T(8,128)S(1)}, f32[64,1024]{1,0:T(8,128)}, u32[]{:S(2)}) copy-start(f32[64,1024]{1,0:T(8,128)} %q_ref.1) | copy-start | bytes 786436
  54.0 14.9 %copy-start.6 = (bf16[768,1024]{1,0:T(8,128)(2,1)S(1)}, bf16[768,1024]{1,0:T(8,128)(2,1)}, u32[]{:S(2)}) copy-start(bf16[768,1024]{1,0:T(8,128)(2,1)} %constant.11.clone.tl_ref) | copy-start | bytes 4718596
  54.0 14.8 %copy-start.8 = (bf16[768,1024]{1,0:T(8,128)(2,1)S(1)}, bf16[768,1024]{1,0:T(8,128)(2,1)}, u32[]{:S(2)}) copy-start(bf16[768,1024]{1,0:T(8,128)(2,1)} %constant.10.clone.th_ref) | copy-start | bytes 4718596

commit v2 on v0

v2 whole, which is shorter than its diff:
```python
import functools, math
import numpy as np
import jax
import jax.numpy as jnp
from jax import lax
from jax.experimental import pallas as pl
from jax.experimental.pallas import tpu as pltpu
from jax.sharding import Mesh
from jax.sharding import PartitionSpec as P

F32, BF16 = jnp.float32, jnp.bfloat16
LANES = 128

BAND = ("band_0", "band_1", "band_2")
MEMBER_BAND = ("member",) + BAND


def trig_table(cells, coeffs):
    half = coeffs // 2
    position = np.arange(cells)[:, None]
    column = np.arange(coeffs)[None, :]
    turns = position * (column % half) % cells
    angles = turns * (2.0 * np.pi / cells)
    return np.where(column < half, np.cos(angles), np.sin(angles)).astype(np.float32)


def split_table(table):
    high = table.astype(jnp.bfloat16)
    low = (table - high.astype(np.float32)).astype(jnp.bfloat16)
    return high, low


def split(value):
    high = value.astype(BF16)
    return high, (value - high.astype(F32)).astype(BF16)


def dot(a, b):
    return jnp.dot(a, b, preferred_element_type=F32)


def dot3(a_high, a_low, b_high, b_low):
    return dot(a_high, b_high) + dot(a_low, b_high) + dot(a_high, b_low)


def lane_halves(shape):
    return lax.broadcasted_iota(jnp.int32, shape, 1) < LANES // 2


def swap(a, b):
    left = lane_halves(a.shape)
    return (
        jnp.where(left, a, pltpu.roll(b, LANES // 2, 1)),
        jnp.where(left, pltpu.roll(a, LANES // 2, 1), b),
    )


def synth_y(levels, rows, x_ref, th_ref, tl_ref, o_ref, xh, xl, acc):
    @pl.when(pl.program_id(0) == 0)
    def _():
        high, low = split(x_ref[...].reshape(levels * rows, x_ref.shape[2]))
        xh[...] = high
        xl[...] = low

    acc[...] = dot3(xh[...], xl[...], th_ref[...], tl_ref[...])
    for p in range(levels // 2):
        for h in range(2):
            a = acc[2 * p * rows : (2 * p + 1) * rows, h * LANES : (h + 1) * LANES]
            b = acc[(2 * p + 1) * rows : (2 * p + 2) * rows, h * LANES : (h + 1) * LANES]
            even, odd = swap(a, b)
            o_ref[2 * h, p] = even
            o_ref[2 * h + 1, p] = odd


def reversed_rows(block, fill):
    count = block.shape[0]
    row = lax.broadcasted_iota(jnp.int32, (count, count), 0)
    col = lax.broadcasted_iota(jnp.int32, (count, count), 1)
    flip = jnp.where(row + col == count, 1.0, 0.0).astype(BF16)
    high = block.astype(BF16)
    rest = block - high.astype(F32)
    middle = rest.astype(BF16)
    low = (rest - middle.astype(F32)).astype(BF16)
    turned = dot(flip, high) + dot(flip, middle) + dot(flip, low)
    return first_row(turned, fill)


def first_row(block, fill):
    row = lax.broadcasted_iota(jnp.int32, block.shape, 0)
    return jnp.where(row == 0, fill, block)


def folded_field(a, out):
    turned = jnp.concatenate([a, a], axis=0).T
    q = turned.shape[0] // 4
    out[0:q] = turned[0:q]
    out[q : 2 * q] = reversed_rows(turned[q : 2 * q], turned[2 * q : 2 * q + 1])
    out[2 * q : 3 * q] = reversed_rows(turned[3 * q :], turned[q : q + 1])
    out[3 * q :] = first_row(turned[2 * q : 3 * q], turned[3 * q : 3 * q + 1])


def alternate(count):
    row = lax.broadcasted_iota(jnp.int32, (count, 1), 0)
    return jnp.where(row % 2 == 0, 1.0, -1.0).astype(F32)


SUB = 64


def synth_x(r_ref, th_ref, tl_ref, c_ref, p_ref, e_ref, rh, rl, basis, field):
    bands, groups, rows, _ = r_ref.shape
    n = groups * LANES
    few = rows // 2
    quarter = th_ref.shape[1]
    folded_field(c_ref[...] * (1.0 / (bands * rows // 2)), field)
    corner = {f: [jnp.zeros((1, LANES), F32)] * groups for f in (0, 3)}
    for f in range(4):
        for i in range(bands // 4):
            s = (f // 2) * (bands // 2) + 2 * i
            for g in range(groups):
                lanes = slice(g * LANES, (g + 1) * LANES)
                part = jnp.concatenate([r_ref[s + t, g, pl.ds(f % 2, few, 2), :] for t in range(2)], axis=0)
                if f in corner:
                    corner[f][g] += jnp.sum(part * alternate(rows), axis=0, keepdims=True)
                high, low = split(part)
                rh[f, i * rows : (i + 1) * rows, lanes] = high
                rl[f, i * rows : (i + 1) * rows, lanes] = low
    e_ref[...] = jnp.zeros_like(e_ref)
    for j in range(n // 256):
        cols = slice(j * 256, (j + 1) * 256)
        for f in range(4):
            basis[f] = dot3(th_ref[f], tl_ref[f], rh[f, :, cols], rl[f, :, cols])
        for h in range(2):
            lanes = slice(h * LANES, (h + 1) * LANES)
            target = slice(j * 256 + h * LANES, j * 256 + (h + 1) * LANES)
            total = jnp.zeros((1, LANES), F32)
            for r in range(0, quarter, SUB):
                ce, co, se, so = (basis[f, r : r + SUB, lanes] for f in range(4))
                plus, minus, both, less = ce + co, ce - co, se + so, so - se
                blocks = [plus + both, minus + less, plus - both, minus - less]
                if r == 0:
                    blocks[2] = first_row(blocks[2], corner[0][2 * j + h] + corner[3][2 * j + h])
                    blocks[3] = first_row(blocks[3], corner[0][2 * j + h] - corner[3][2 * j + h])
                for b, block in enumerate(blocks):
                    at = slice(b * quarter + r, b * quarter + r + SUB)
                    product = block * field[at, :]
                    p_ref[at, target] = product
                    total += jnp.sum(product * product, axis=0, keepdims=True)
            for d in range(e_ref.shape[0]):
                e_ref[d, 2 * j + h : 2 * j + h + 1, :] = total


def group_sum(v):
    lane = lax.broadcasted_iota(jnp.int32, v.shape, 1)
    step = 1
    while step < LANES // 2:
        v = v + jnp.where(lane % (2 * step) < step, pltpu.roll(v, LANES - step, 1), pltpu.roll(v, step, 1))
        step *= 2
    return v


def analyse_x(points, p_ref, e_ref, q_ref, th_ref, tl_ref, o_ref, gh, gl, corners, field):
    bands, groups, rows, _ = o_ref.shape
    n = groups * LANES
    few = rows // 2
    coeffs, quarter = th_ref.shape[1], th_ref.shape[2]
    folded_field(q_ref[...], field)
    total = group_sum(jnp.sum(e_ref[...], axis=0))
    scale = lax.rsqrt(total * (1.0 / points) + 1e-06)
    for t in range(n // LANES):
        lanes = slice(t * LANES, (t + 1) * LANES)
        for r in range(0, quarter, SUB):
            g = []
            for b in range(4):
                at = slice(b * quarter + r, b * quarter + r + SUB)
                scaled = p_ref[at, lanes] * scale[t : t + 1, :]
                g.append(scaled + field[at, :] * scaled * scaled)
            sum0, less0, sum1, less1 = g[0] + g[1], g[0] - g[1], g[2] + g[3], g[2] - g[3]
            folded = [sum0 + sum1, less0 + less1, less0 - less1, sum0 - sum1]
            if r == 0:
                corners[0:1, lanes] = sum1[0:1]
                corners[1:2, lanes] = less1[0:1]
                folded[0] = first_row(folded[0], sum0[0:1])
                folded[1] = first_row(folded[1], less0[0:1])
            for f in range(4):
                high, low = split(folded[f])
                gh[f, r : r + SUB, lanes] = high
                gl[f, r : r + SUB, lanes] = low
    row = lax.broadcasted_iota(jnp.int32, (coeffs, 1), 0)
    for j in range(n // 256):
        cols = slice(j * 256, (j + 1) * 256)
        for f in range(4):
            value = dot3(th_ref[f], tl_ref[f], gh[f, :, cols], gl[f, :, cols])
            if f in (0, 3):
                value += alternate(coeffs) * corners[f // 3 : f // 3 + 1, cols]
            value *= jnp.where(row == 0, 1.0 if f == 0 else 2.0, 2.0).astype(F32)
            for i in range(bands // 2):
                for h in range(2):
                    o_ref[(f // 2) * (bands // 2) + i, 2 * j + h, pl.ds(f % 2, few, 2), :] = value[
                        i * few : (i + 1) * few, h * LANES : (h + 1) * LANES
                    ]


def analyse_y(levels, factor, r_ref, th_ref, tl_ref, o_ref, yh, yl):
    bands, rows = r_ref.shape[0], r_ref.shape[2]
    for p in range(levels // 2):
        for s in range(bands // 2):
            a = r_ref[2 * s, p]
            b = r_ref[2 * s + 1, p]
            for i, piece in enumerate(swap(a, b)):
                high, low = split(piece)
                at = (2 * p + i) * rows
                yh[at : at + rows, s * LANES : (s + 1) * LANES] = high
                yl[at : at + rows, s * LANES : (s + 1) * LANES] = low
    coeffs = th_ref.shape[1]
    for j in range(coeffs // 256):
        cols = slice(j * 256, (j + 1) * 256)
        col = j * 256 + lax.broadcasted_iota(jnp.int32, (1, 256), 1)
        weight = jnp.where(col % (coeffs // 2) == 0, factor, 2.0 * factor).astype(F32)
        value = dot3(yh[...], yl[...], th_ref[:, cols], tl_ref[:, cols]) * weight
        o_ref[:, :, cols] = value.reshape(levels, rows, 256)


def stage(kernel, in_specs, out_shape, scratch, flops, nbytes, limit=16):
    return pl.pallas_call(
        kernel,
        in_specs=[pl.BlockSpec(memory_space=m) for m in in_specs],
        out_shape=out_shape,
        scratch_shapes=scratch,
        compiler_params=pltpu.CompilerParams(vmem_limit_bytes=limit * 1024 * 1024),
        cost_estimate=pl.CostEstimate(flops=flops, bytes_accessed=nbytes, transcendentals=0),
    )


def on_device(bands, spectral, coupling, quadratic):
    levels, rows, coeffs = spectral.shape
    own, cells = coupling.shape
    quarter = cells // 4
    table = trig_table(cells, coeffs)
    th, tl = (jnp.asarray(t) for t in split_table(table))
    yh, yl = (jnp.asarray(np.stack(np.split(t, 4, 1))) for t in split_table(np.ascontiguousarray(table.T)))
    folds = np.stack([table[:quarter, f // 2 * (coeffs // 2) + f % 2 :: 2][:, : coeffs // 4] for f in range(4)])
    fh, fl = (jnp.asarray(t) for t in split_table(folds))
    bh, bl = (jnp.asarray(t) for t in split_table(np.ascontiguousarray(folds.transpose(0, 2, 1))))
    n = levels * own
    flops = 6 * n * cells * coeffs
    nbytes = 4 * n * (cells + coeffs) + 4 * cells * coeffs
    factor = (coeffs // 2) / float(cells * cells)
    spread = jax.ShapeDtypeStruct((bands, n // LANES, rows, LANES), F32)
    vmem = pltpu.VMEM

    def exchange(a):
        return lax.all_to_all(a, BAND, 0, 0, tiled=True)

    first = pl.pallas_call(
        functools.partial(synth_y, levels, rows),
        grid=(bands // 4,),
        in_specs=[
            pl.BlockSpec((levels, rows, coeffs), lambda j: (0, 0, 0)),
            pl.BlockSpec((None, coeffs, 256), lambda j: (j, 0, 0)),
            pl.BlockSpec((None, coeffs, 256), lambda j: (j, 0, 0)),
        ],
        out_specs=pl.BlockSpec((4, n // LANES, rows, LANES), lambda j: (j, 0, 0, 0)),
        out_shape=spread,
        scratch_shapes=[vmem((levels * rows, coeffs), BF16)] * 2 + [vmem((levels * rows, 256), F32)],
        compiler_params=pltpu.CompilerParams(vmem_limit_bytes=60 * 1024 * 1024),
        cost_estimate=pl.CostEstimate(flops=flops, bytes_accessed=nbytes, transcendentals=0),
    )
    second = stage(
        synth_x, [vmem] * 4,
        (jax.ShapeDtypeStruct((cells, n), F32), jax.ShapeDtypeStruct((bands, 8, LANES), F32)),
        [vmem((4, coeffs // 4, n), BF16)] * 2 + [vmem((4, quarter, 256), F32), vmem((cells, LANES), F32)],
        flops, nbytes,
    )
    third = stage(
        functools.partial(analyse_x, float(cells * cells)), [vmem] * 5, spread,
        [vmem((4, quarter, n), BF16)] * 2 + [vmem((8, n), F32), vmem((cells, LANES), F32)],
        flops, nbytes,
    )
    fourth = stage(
        functools.partial(analyse_y, levels, factor), [vmem] * 3,
        jax.ShapeDtypeStruct((levels, rows, coeffs), F32),
        [vmem((levels * rows, cells), BF16)] * 2,
        flops, nbytes,
    )
    turned = exchange(first(spectral, yh, yl))
    product, energy = second(turned, fh, fl, coupling)
    back = exchange(third(product, exchange(energy), quadratic, bh, bl))
    return fourth(back, th, tl)


def solution(mesh):
    torus = Mesh(
        mesh.devices.reshape(mesh.shape["member"], 2, 4, 2),
        ("member",) + BAND,
    )
    return jax.shard_map(
        functools.partial(on_device, mesh.shape["band"]),
        mesh=torus,
        in_specs=(P("member", BAND, None), P(MEMBER_BAND, None), P(MEMBER_BAND, None)),
        out_specs=P("member", BAND, None),
        check_vma=False,
    )
```

time: 140 us -> 117 us (0.84)
  blocking collectives: 40.8 us -> 95.1 us
  waiting for transfers between devices: 41.2 us -> 0 us
  local copies, waits for them, and re-layouts: 19.9 us -> 0.04 us
  starting transfers between devices: 11.5 us -> 0 us
  other arithmetic: 3.49 us -> 0 us
    all_to_all x1 -> x3, blocking collectives: 40.8 us -> 95.1 us  [exchange(): return lax.all_to_all(a, BAND, 0, 0, tiled=True)]
    all_to_all x2 -> x0, waiting for transfers between devices: 41.2 us -> none  [exchange(): return lax.all_to_all(a, BAND, 0, 0, tiled=True)]
    unnamed x30 -> x16, local copies, waits for them, and re-layouts: 19.9 us -> 0.04 us
    all_to_all x2 -> x0, starting transfers between devices: 11.5 us -> none  [exchange(): return lax.all_to_all(a, BAND, 0, 0, tiled=True)]
    concatenate x2 -> x0, other arithmetic: 2.4 us -> none  [the longest x1 1.4 us: on_device(): qt = jnp.concatenate([quadratic.T, quadratic.T], axis=1)]
  transfers between devices with their start and end apart: 2 -> 0, of which waited for: 2 -> 0; matrix products, arithmetic and copies ran while one was open for 5% -> 0% of each run, Pallas kernels for 0% -> 0%
where the time goes in v2:
time: 117 us
  blocking collectives  95.1 us (81%)
  Pallas kernels  21.5 us (18%)
    all_to_all x3, blocking collectives, exchange(): return lax.all_to_all(a, BAND, 0, 0, tiled=True)  95.1 us
    pallas_call x1, Pallas kernels, on_device(): turned = exchange(first(spectral, yh, yl))  8.1 us
    pallas_call x1, Pallas kernels, on_device(): return fourth(back, th, tl)  5.82 us
    pallas_call x1, Pallas kernels, on_device(): back = exchange(third(product, exchange(energy), quadratic, bh, bl))  4.59 us
    pallas_call x1, Pallas kernels, on_device(): product, energy = second(turned, fh, fl, coupling)  2.97 us

profile of v2, /device:TPU:1, one launch (start us, length us, event | category | flops | bytes accessed | tf_op | source)
XLA Modules:
  0.0 116.7 jit_solution(17567196708775947371)
XLA Ops:
  0.0 8.1 %shard_map.109 = f32[16,8,48,128]{3,2,1,0:T(8,128)} custom-call(f32[16,48,768]{2,1,0:T(8,128)} %x_ref.1, bf16[4,768,256]{2,1,0:T(8,128)(2,1)} %constant.18.clone.th_ref, bf16[4,768,256]{2,1,0:T(8,128)(2,1)} %constant.19.clone.tl_ref), custom_call_target="tpu_custom_call" | custom-call | flops 4831838208 | bytes 10485760 | tf_op jit(solution)/shard_map/pallas_call | solution.py:286
  8.1 0.0 copy-start
  8.1 0.0 copy-start.4
  8.1 0.0 copy-start.5
  8.1 44.5 %all_to_all.15.r_ref = f32[16,8,48,128]{3,2,1,0:T(8,128)S(1)} all-to-all(f32[16,8,48,128]{3,2,1,0:T(8,128)} %shard_map.109), channel_id=1, replica_groups=mesh['member'=16,'band_0'=2,'band_1'=4,'band_2'=2] {'band_0','band_1','b..., dimensions={0} | all-to-all | bytes 6291456 | tf_op jit(solution)/shard_map/all_to_all | solution.py:253
  52.6 0.0 copy-done
  52.7 0.0 copy-done.4
  52.7 0.0 copy-done.5
  52.7 0.0 copy-start.1
  52.7 0.0 copy-start.6
  52.7 0.0 copy-start.7
  52.7 3.0 %shard_map.110 = (f32[1024,1024]{1,0:T(8,128)S(1)}, f32[16,8,128]{2,1,0:T(8,128)S(1)}) custom-call(f32[16,8,48,128]{3,2,1,0:T(8,128)S(1)} %all_to_all.15.r_ref, bf16[4,256,192]{2,1,0:T(8,128)(2,1)S(1)} %copy-done.5, bf16[4,256,192]{2,1,0:T(8,128)(2,1)S(1)} %copy-done.4, f32[64,1024]{1,0:T(8,128)S(1)} %copy-done), custom_call_target="tpu_custom_call" | custom-call | flops 4831838208 | bytes 10485760 | tf_op jit(solution)/shard_map/pallas_call | solution.py:287
  55.7 9.7 %all_to_all.16.e_ref = f32[16,8,128]{2,1,0:T(8,128)S(1)} all-to-all(f32[16,8,128]{2,1,0:T(8,128)S(1)} %get-tuple-element.8), channel_id=1, replica_groups=mesh['member'=16,'band_0'=2,'band_1'=4,'band_2'=2] {'band_0','band_1','b..., dimensions={0} | all-to-all | bytes 131072 | tf_op jit(solution)/shard_map/all_to_all | solution.py:253
  65.4 0.0 copy-done.1
  65.4 0.0 copy-done.6
  65.4 0.0 copy-done.7
  65.4 4.6 %shard_map.111 = f32[16,8,48,128]{3,2,1,0:T(8,128)S(1)} custom-call(f32[1024,1024]{1,0:T(8,128)S(1)} %get-tuple-element.7.p_ref, f32[16,8,128]{2,1,0:T(8,128)S(1)} %all_to_all.16.e_ref, f32[64,1024]{1,0:T(8,128)S(1)} %copy-done.1, bf16[4,192,256]{2,1,0:T(8,128)(2,1)S(1)} %copy-done.7, bf16[4,192,256]{2,1,0:T(8,128)(2,1)S(1)} %copy-done.6), custom_call_target="tpu_custom_call" | custom-call | flops 4831838208 | bytes 10485760 | tf_op jit(solution)/shard_map/pallas_call | solution.py:288
  70.0 0.0 copy-start.2
  70.0 0.0 copy-start.3
  70.0 40.8 %all_to_all.17.r_ref = f32[16,8,48,128]{3,2,1,0:T(8,128)S(1)} all-to-all(f32[16,8,48,128]{3,2,1,0:T(8,128)S(1)} %shard_map.111), channel_id=1, replica_groups=mesh['member'=16,'band_0'=2,'band_1'=4,'band_2'=2] {'band_0','band_1','b..., dimensions={0} | all-to-all | bytes 6291456 | tf_op jit(solution)/shard_map/all_to_all | solution.py:253
  110.8 0.0 copy-done.2
  110.8 0.0 copy-done.3
  110.8 5.8 %shard_map.112 = f32[16,48,768]{2,1,0:T(8,128)} custom-call(f32[16,8,48,128]{3,2,1,0:T(8,128)S(1)} %all_to_all.17.r_ref, bf16[1024,768]{1,0:T(8,128)(2,1)S(1)} %copy-done.3, bf16[1024,768]{1,0:T(8,128)(2,1)S(1)} %copy-done.2), custom_call_target="tpu_custom_call" | custom-call | flops 4831838208 | bytes 10485760 | tf_op jit(solution)/shard_map/pallas_call | solution.py:289
Async XLA Ops:
  8.1 44.5 %copy-start = (f32[64,1024]{1,0:T(8,128)S(1)}, f32[64,1024]{1,0:T(8,128)}, u32[]{:S(2)}) copy-start(f32[64,1024]{1,0:T(8,128)} %c_ref.1) | copy-start | bytes 786436
  8.1 44.5 %copy-start.4 = (bf16[4,256,192]{2,1,0:T(8,128)(2,1)S(1)}, bf16[4,256,192]{2,1,0:T(8,128)(2,1)}, u32[]{:S(2)}) copy-start(bf16[4,256,192]{2,1,0:T(8,128)(2,1)} %constant.21.clone.tl_ref) | copy-start | bytes 1179652
  8.1 44.6 %copy-start.5 = (bf16[4,256,192]{2,1,0:T(8,128)(2,1)S(1)}, bf16[4,256,192]{2,1,0:T(8,128)(2,1)}, u32[]{:S(2)}) copy-start(bf16[4,256,192]{2,1,0:T(8,128)(2,1)} %constant.20.clone.th_ref) | copy-start | bytes 1179652
  52.7 12.7 %copy-start.1 = (f32[64,1024]{1,0:T(8,128)S(1)}, f32[64,1024]{1,0:T(8,128)}, u32[]{:S(2)}) copy-start(f32[64,1024]{1,0:T(8,128)} %q_ref.1) | copy-start | bytes 786436
  52.7 12.7 %copy-start.6 = (bf16[4,192,256]{2,1,0:T(8,128)(2,1)S(1)}, bf16[4,192,256]{2,1,0:T(8,128)(2,1)}, u32[]{:S(2)}) copy-start(bf16[4,192,256]{2,1,0:T(8,128)(2,1)} %constant.23.clone.tl_ref) | copy-start | bytes 1179652
  52.7 12.7 %copy-start.7 = (bf16[4,192,256]{2,1,0:T(8,128)(2,1)S(1)}, bf16[4,192,256]{2,1,0:T(8,128)(2,1)}, u32[]{:S(2)}) copy-start(bf16[4,192,256]{2,1,0:T(8,128)(2,1)} %constant.22.clone.th_ref) | copy-start | bytes 1179652
  70.0 40.8 %copy-start.2 = (bf16[1024,768]{1,0:T(8,128)(2,1)S(1)}, bf16[1024,768]{1,0:T(8,128)(2,1)}, u32[]{:S(2)}) copy-start(bf16[1024,768]{1,0:T(8,128)(2,1)} %constant.17.clone.tl_ref) | copy-start | bytes 4718596
  70.0 40.8 %copy-start.3 = (bf16[1024,768]{1,0:T(8,128)(2,1)S(1)}, bf16[1024,768]{1,0:T(8,128)(2,1)}, u32[]{:S(2)}) copy-start(bf16[1024,768]{1,0:T(8,128)(2,1)} %constant.16.clone.th_ref) | copy-start | bytes 4718596

commit v3 on v2

--- a/solution.py
+++ b/solution.py
@@ -72,17 +72,30 @@
             o_ref[2 * h + 1, p] = odd
 
 
+def picked(choice, value):
+    choice = jnp.where(choice, 1.0, 0.0).astype(BF16)
+    high = value.astype(BF16)
+    rest = value - high.astype(F32)
+    middle = rest.astype(BF16)
+    low = (rest - middle.astype(F32)).astype(BF16)
+    return dot(choice, high) + dot(choice, middle) + dot(choice, low)
+
+
+def positions(count):
+    return tuple(lax.broadcasted_iota(jnp.int32, (count, count), d) for d in range(2))
+
+
 def reversed_rows(block, fill):
     count = block.shape[0]
-    row = lax.broadcasted_iota(jnp.int32, (count, count), 0)
-    col = lax.broadcasted_iota(jnp.int32, (count, count), 1)
-    flip = jnp.where(row + col == count, 1.0, 0.0).astype(BF16)
-    high = block.astype(BF16)
-    rest = block - high.astype(F32)
-    middle = rest.astype(BF16)
-    low = (rest - middle.astype(F32)).astype(BF16)
-    turned = dot(flip, high) + dot(flip, middle) + dot(flip, low)
-    return first_row(turned, fill)
+    row, col = positions(count)
+    return first_row(picked(row + col == count, block), fill)
+
+
+def band_order(a):
+    count = a.shape[0]
+    row, col = positions(count)
+    upper = lax.axis_index(BAND[0])
+    return picked(col == row + upper * (count - 1 - 2 * row), a)
 
 
 def first_row(block, fill):
@@ -91,6 +104,7 @@
 
 
 def folded_field(a, out):
+    a = band_order(a)
     turned = jnp.concatenate([a, a], axis=0).T
     q = turned.shape[0] // 4
     out[0:q] = turned[0:q]
@@ -105,6 +119,7 @@
 
 
 SUB = 64
+PIECES = 4
 
 
 def synth_x(r_ref, th_ref, tl_ref, c_ref, p_ref, e_ref, rh, rl, basis, field):
@@ -201,33 +216,53 @@
                     ]
 
 
-def analyse_y(levels, factor, r_ref, th_ref, tl_ref, o_ref, yh, yl):
+def analyse_y(levels, factor, r_ref, th_ref, tl_ref, o_hbm, yh, yl, edge, o_ref, sem):
     bands, rows = r_ref.shape[0], r_ref.shape[2]
-    for p in range(levels // 2):
-        for s in range(bands // 2):
-            a = r_ref[2 * s, p]
-            b = r_ref[2 * s + 1, p]
-            for i, piece in enumerate(swap(a, b)):
-                high, low = split(piece)
-                at = (2 * p + i) * rows
-                yh[at : at + rows, s * LANES : (s + 1) * LANES] = high
-                yl[at : at + rows, s * LANES : (s + 1) * LANES] = low
-    coeffs = th_ref.shape[1]
-    for j in range(coeffs // 256):
-        cols = slice(j * 256, (j + 1) * 256)
-        col = j * 256 + lax.broadcasted_iota(jnp.int32, (1, 256), 1)
-        weight = jnp.where(col % (coeffs // 2) == 0, factor, 2.0 * factor).astype(F32)
-        value = dot3(yh[...], yl[...], th_ref[:, cols], tl_ref[:, cols]) * weight
-        o_ref[:, :, cols] = value.reshape(levels, rows, 256)
-
-
-def stage(kernel, in_specs, out_shape, scratch, flops, nbytes, limit=16):
+    half = th_ref.shape[2]
+    start = lax.broadcasted_iota(jnp.int32, (rows, LANES), 1) == 0
+    col = lax.broadcasted_iota(jnp.int32, (1, half), 1)
+    weight = jnp.where(col == 0, factor, 2.0 * factor).astype(F32)
+    pieces = sem.shape[0]
+    step = levels // pieces
+    copies = []
+    for g in range(pieces):
+        for p in range(g * step // 2, (g + 1) * step // 2):
+            before = [jnp.zeros((rows, LANES), F32)] * 2
+            for s in range(bands // 4):
+                lower = swap(r_ref[2 * s, p], r_ref[2 * s + 1, p])
+                upper = swap(r_ref[bands - 1 - 2 * s, p], r_ref[bands - 2 - 2 * s, p])
+                for i in range(2):
+                    at = slice((2 * p + i) * rows, (2 * p + i + 1) * rows)
+                    shifted = pltpu.roll(upper[i], 1, 1)
+                    mirror = jnp.where(start, before[i], shifted)
+                    before[i] = shifted
+                    for f, value in enumerate((lower[i] + mirror, lower[i] - mirror)):
+                        high, low = split(value)
+                        yh[f, at, s * LANES : (s + 1) * LANES] = high
+                        yl[f, at, s * LANES : (s + 1) * LANES] = low
+            for i in range(2):
+                edge[(2 * p + i) * rows : (2 * p + i + 1) * rows, :] = before[i]
+        at = slice(g * step * rows, (g + 1) * step * rows)
+        for f in range(2):
+            value = dot3(yh[f, at], yl[f, at], th_ref[f], tl_ref[f])
+            if f == 0:
+                value += edge[at, 0:1] * jnp.where(col % 2 == 0, 1.0, -1.0).astype(F32)
+            o_ref[g * step : (g + 1) * step, :, f * half : (f + 1) * half] = (value * weight).reshape(step, rows, half)
+        part = pl.ds(g * step, step)
+        copies.append(pltpu.make_async_copy(o_ref.at[part], o_hbm.at[part], sem.at[g]))
+        copies[-1].start()
+    for copy in copies:
+        copy.wait()
+
+
+def stage(kernel, in_specs, out_shape, scratch, flops, nbytes, out_specs=None):
     return pl.pallas_call(
         kernel,
         in_specs=[pl.BlockSpec(memory_space=m) for m in in_specs],
+        **({} if out_specs is None else {"out_specs": out_specs}),
         out_shape=out_shape,
         scratch_shapes=scratch,
-        compiler_params=pltpu.CompilerParams(vmem_limit_bytes=limit * 1024 * 1024),
+        compiler_params=pltpu.CompilerParams(vmem_limit_bytes=16 * 1024 * 1024),
         cost_estimate=pl.CostEstimate(flops=flops, bytes_accessed=nbytes, transcendentals=0),
     )
 
@@ -237,8 +272,12 @@
     own, cells = coupling.shape
     quarter = cells // 4
     table = trig_table(cells, coeffs)
-    th, tl = (jnp.asarray(t) for t in split_table(table))
-    yh, yl = (jnp.asarray(np.stack(np.split(t, 4, 1))) for t in split_table(np.ascontiguousarray(table.T)))
+    halves = np.stack([table[: cells // 2, : coeffs // 2], table[: cells // 2, coeffs // 2 :]])
+    th, tl = (jnp.asarray(t) for t in split_table(halves))
+    order = np.arange(cells).reshape(bands, own)
+    order[bands // 2 :] = order[bands // 2 :, ::-1]
+    ordered = np.ascontiguousarray(table[order.reshape(-1)].T)
+    yh, yl = (jnp.asarray(np.stack(np.split(t, 4, 1))) for t in split_table(ordered))
     folds = np.stack([table[:quarter, f // 2 * (coeffs // 2) + f % 2 :: 2][:, : coeffs // 4] for f in range(4)])
     fh, fl = (jnp.asarray(t) for t in split_table(folds))
     bh, bl = (jnp.asarray(t) for t in split_table(np.ascontiguousarray(folds.transpose(0, 2, 1))))
@@ -280,8 +319,10 @@
     fourth = stage(
         functools.partial(analyse_y, levels, factor), [vmem] * 3,
         jax.ShapeDtypeStruct((levels, rows, coeffs), F32),
-        [vmem((levels * rows, cells), BF16)] * 2,
-        flops, nbytes,
+        [vmem((2, levels * rows, cells // 2), BF16)] * 2 + [
+            vmem((levels * rows, LANES), F32), vmem((levels, rows, coeffs), F32), pltpu.SemaphoreType.DMA((PIECES,))
+        ],
+        flops, nbytes, pl.BlockSpec(memory_space=pl.ANY),
     )
     turned = exchange(first(spectral, yh, yl))
     product, energy = second(turned, fh, fl, coupling)

time: 117 us -> 115 us (0.983)
  Pallas kernels: 21.5 us -> 19.9 us
    pallas_call x1, Pallas kernels: 5.82 us -> 3.86 us  [on_device(): return fourth(back, th, tl)]
where the time goes in v3:
time: 115 us
  blocking collectives  94.9 us (83%)
  Pallas kernels  19.9 us (17%)
    all_to_all x3, blocking collectives, exchange(): return lax.all_to_all(a, BAND, 0, 0, tiled=True)  94.9 us
    pallas_call x1, Pallas kernels, on_device(): turned = exchange(first(spectral, yh, yl))  8.1 us
    pallas_call x1, Pallas kernels, on_device(): back = exchange(third(product, exchange(energy), quadratic, bh, bl))  4.8 us
    pallas_call x1, Pallas kernels, on_device(): return fourth(back, th, tl)  3.86 us
    pallas_call x1, Pallas kernels, on_device(): product, energy = second(turned, fh, fl, coupling)  3.18 us

profile of v3, /device:TPU:1, one launch (start us, length us, event | category | flops | bytes accessed | tf_op | source)
XLA Modules:
  0.0 115.2 jit_solution(15138657594014710979)
XLA Ops:
  0.0 8.1 %shard_map.109 = f32[16,8,48,128]{3,2,1,0:T(8,128)} custom-call(f32[16,48,768]{2,1,0:T(8,128)} %x_ref.1, bf16[4,768,256]{2,1,0:T(8,128)(2,1)} %constant.18.clone.th_ref, bf16[4,768,256]{2,1,0:T(8,128)(2,1)} %constant.19.clone.tl_ref), custom_call_target="tpu_custom_call" | custom-call | flops 4831838208 | bytes 10485760 | tf_op jit(solution)/shard_map/pallas_call | solution.py:327
  8.1 0.0 copy-start
  8.1 0.0 copy-start.4
  8.1 0.0 copy-start.5
  8.1 44.5 %all_to_all.15.r_ref = f32[16,8,48,128]{3,2,1,0:T(8,128)S(1)} all-to-all(f32[16,8,48,128]{3,2,1,0:T(8,128)} %shard_map.109), channel_id=1, replica_groups=mesh['member'=16,'band_0'=2,'band_1'=4,'band_2'=2] {'band_0','band_1','b..., dimensions={0} | all-to-all | bytes 6291456 | tf_op jit(solution)/shard_map/all_to_all | solution.py:292
  52.6 0.0 copy-done
  52.7 0.0 copy-done.4
  52.7 0.0 copy-done.5
  52.7 0.0 copy-start.1
  52.7 0.0 copy-start.6
  52.7 0.0 copy-start.7
  52.7 3.2 %shard_map.110 = (f32[1024,1024]{1,0:T(8,128)S(1)}, f32[16,8,128]{2,1,0:T(8,128)S(1)}) custom-call(f32[16,8,48,128]{3,2,1,0:T(8,128)S(1)} %all_to_all.15.r_ref, bf16[4,256,192]{2,1,0:T(8,128)(2,1)S(1)} %copy-done.5, bf16[4,256,192]{2,1,0:T(8,128)(2,1)S(1)} %copy-done.4, f32[64,1024]{1,0:T(8,128)S(1)} %copy-done), custom_call_target="tpu_custom_call" | custom-call | flops 4831838208 | bytes 10485760 | tf_op jit(solution)/shard_map/pallas_call | solution.py:328
  55.9 9.7 %all_to_all.16.e_ref = f32[16,8,128]{2,1,0:T(8,128)S(1)} all-to-all(f32[16,8,128]{2,1,0:T(8,128)S(1)} %get-tuple-element.8), channel_id=1, replica_groups=mesh['member'=16,'band_0'=2,'band_1'=4,'band_2'=2] {'band_0','band_1','b..., dimensions={0} | all-to-all | bytes 131072 | tf_op jit(solution)/shard_map/all_to_all | solution.py:292
  65.6 0.0 copy-done.1
  65.6 0.0 copy-done.6
  65.6 0.0 copy-done.7
  65.6 4.8 %shard_map.111 = f32[16,8,48,128]{3,2,1,0:T(8,128)S(1)} custom-call(f32[1024,1024]{1,0:T(8,128)S(1)} %get-tuple-element.7.p_ref, f32[16,8,128]{2,1,0:T(8,128)S(1)} %all_to_all.16.e_ref, f32[64,1024]{1,0:T(8,128)S(1)} %copy-done.1, bf16[4,192,256]{2,1,0:T(8,128)(2,1)S(1)} %copy-done.7, bf16[4,192,256]{2,1,0:T(8,128)(2,1)S(1)} %copy-done.6), custom_call_target="tpu_custom_call" | custom-call | flops 4831838208 | bytes 10485760 | tf_op jit(solution)/shard_map/pallas_call | solution.py:329
  70.4 0.0 copy-start.2
  70.4 0.0 copy-start.3
  70.5 40.7 %all_to_all.17.r_ref = f32[16,8,48,128]{3,2,1,0:T(8,128)S(1)} all-to-all(f32[16,8,48,128]{3,2,1,0:T(8,128)S(1)} %shard_map.111), channel_id=1, replica_groups=mesh['member'=16,'band_0'=2,'band_1'=4,'band_2'=2] {'band_0','band_1','b..., dimensions={0} | all-to-all | bytes 6291456 | tf_op jit(solution)/shard_map/all_to_all | solution.py:292
  111.1 0.0 copy-done.2
  111.1 0.0 copy-done.3
  111.1 3.9 %shard_map.112 = f32[16,48,768]{2,1,0:T(8,128)} custom-call(f32[16,8,48,128]{3,2,1,0:T(8,128)S(1)} %all_to_all.17.r_ref, bf16[2,512,384]{2,1,0:T(8,128)(2,1)S(1)} %copy-done.3, bf16[2,512,384]{2,1,0:T(8,128)(2,1)S(1)} %copy-done.2), custom_call_target="tpu_custom_call" | custom-call | flops 4831838208 | bytes 10485760 | tf_op jit(solution)/shard_map/pallas_call | solution.py:330
Async XLA Ops:
  8.1 44.5 %copy-start = (f32[64,1024]{1,0:T(8,128)S(1)}, f32[64,1024]{1,0:T(8,128)}, u32[]{:S(2)}) copy-start(f32[64,1024]{1,0:T(8,128)} %c_ref.1) | copy-start | bytes 786436
  8.1 44.5 %copy-start.4 = (bf16[4,256,192]{2,1,0:T(8,128)(2,1)S(1)}, bf16[4,256,192]{2,1,0:T(8,128)(2,1)}, u32[]{:S(2)}) copy-start(bf16[4,256,192]{2,1,0:T(8,128)(2,1)} %constant.21.clone.tl_ref) | copy-start | bytes 1179652
  8.1 44.6 %copy-start.5 = (bf16[4,256,192]{2,1,0:T(8,128)(2,1)S(1)}, bf16[4,256,192]{2,1,0:T(8,128)(2,1)}, u32[]{:S(2)}) copy-start(bf16[4,256,192]{2,1,0:T(8,128)(2,1)} %constant.20.clone.th_ref) | copy-start | bytes 1179652
  52.7 12.9 %copy-start.1 = (f32[64,1024]{1,0:T(8,128)S(1)}, f32[64,1024]{1,0:T(8,128)}, u32[]{:S(2)}) copy-start(f32[64,1024]{1,0:T(8,128)} %q_ref.1) | copy-start | bytes 786436
  52.7 12.9 %copy-start.6 = (bf16[4,192,256]{2,1,0:T(8,128)(2,1)S(1)}, bf16[4,192,256]{2,1,0:T(8,128)(2,1)}, u32[]{:S(2)}) copy-start(bf16[4,192,256]{2,1,0:T(8,128)(2,1)} %constant.23.clone.tl_ref) | copy-start | bytes 1179652
  52.7 12.9 %copy-start.7 = (bf16[4,192,256]{2,1,0:T(8,128)(2,1)S(1)}, bf16[4,192,256]{2,1,0:T(8,128)(2,1)}, u32[]{:S(2)}) copy-start(bf16[4,192,256]{2,1,0:T(8,128)(2,1)} %constant.22.clone.th_ref) | copy-start | bytes 1179652
  70.4 40.7 %copy-start.2 = (bf16[2,512,384]{2,1,0:T(8,128)(2,1)S(1)}, bf16[2,512,384]{2,1,0:T(8,128)(2,1)}, u32[]{:S(2)}) copy-start(bf16[2,512,384]{2,1,0:T(8,128)(2,1)} %constant.17.clone.tl_ref) | copy-start | bytes 2359300
  70.4 40.7 %copy-start.3 = (bf16[2,512,384]{2,1,0:T(8,128)(2,1)S(1)}, bf16[2,512,384]{2,1,0:T(8,128)(2,1)}, u32[]{:S(2)}) copy-start(bf16[2,512,384]{2,1,0:T(8,128)(2,1)} %constant.16.clone.th_ref) | copy-start | bytes 2359300

commit v4 on v3

--- a/solution.py
+++ b/solution.py
@@ -119,7 +119,7 @@
 
 
 SUB = 64
-PIECES = 4
+PIECES = 8
 
 
 def synth_x(r_ref, th_ref, tl_ref, c_ref, p_ref, e_ref, rh, rl, basis, field):

time: 115 us -> 116 us (level)
  no operation moved by 1% of the time
where the time goes in v4:
time: 116 us; the launch traced here: 115 us
  blocking collectives  94.9 us (82%)
  Pallas kernels  20.3 us (18%)
    all_to_all x3, blocking collectives, exchange(): return lax.all_to_all(a, BAND, 0, 0, tiled=True)  94.9 us
    pallas_call x1, Pallas kernels, on_device(): turned = exchange(first(spectral, yh, yl))  8.1 us
    pallas_call x1, Pallas kernels, on_device(): back = exchange(third(product, exchange(energy), quadratic, bh, bl))  4.8 us
    pallas_call x1, Pallas kernels, on_device(): return fourth(back, th, tl)  4.19 us
    pallas_call x1, Pallas kernels, on_device(): product, energy = second(turned, fh, fl, coupling)  3.18 us

profile of v4, /device:TPU:1, one launch (start us, length us, event | category | flops | bytes accessed | tf_op | source)
XLA Modules:
  0.0 115.5 jit_solution(9519630227559221502)
XLA Ops:
  0.0 8.1 %shard_map.109 = f32[16,8,48,128]{3,2,1,0:T(8,128)} custom-call(f32[16,48,768]{2,1,0:T(8,128)} %x_ref.1, bf16[4,768,256]{2,1,0:T(8,128)(2,1)} %constant.18.clone.th_ref, bf16[4,768,256]{2,1,0:T(8,128)(2,1)} %constant.19.clone.tl_ref), custom_call_target="tpu_custom_call" | custom-call | flops 4831838208 | bytes 10485760 | tf_op jit(solution)/shard_map/pallas_call | solution.py:327
  8.1 0.0 copy-start
  8.1 0.0 copy-start.4
  8.1 0.0 copy-start.5
  8.1 44.5 %all_to_all.15.r_ref = f32[16,8,48,128]{3,2,1,0:T(8,128)S(1)} all-to-all(f32[16,8,48,128]{3,2,1,0:T(8,128)} %shard_map.109), channel_id=1, replica_groups=mesh['member'=16,'band_0'=2,'band_1'=4,'band_2'=2] {'band_0','band_1','b..., dimensions={0} | all-to-all | bytes 6291456 | tf_op jit(solution)/shard_map/all_to_all | solution.py:292
  52.6 0.0 copy-done
  52.7 0.0 copy-done.4
  52.7 0.0 copy-done.5
  52.7 0.0 copy-start.1
  52.7 0.0 copy-start.6
  52.7 0.0 copy-start.7
  52.7 3.2 %shard_map.110 = (f32[1024,1024]{1,0:T(8,128)S(1)}, f32[16,8,128]{2,1,0:T(8,128)S(1)}) custom-call(f32[16,8,48,128]{3,2,1,0:T(8,128)S(1)} %all_to_all.15.r_ref, bf16[4,256,192]{2,1,0:T(8,128)(2,1)S(1)} %copy-done.5, bf16[4,256,192]{2,1,0:T(8,128)(2,1)S(1)} %copy-done.4, f32[64,1024]{1,0:T(8,128)S(1)} %copy-done), custom_call_target="tpu_custom_call" | custom-call | flops 4831838208 | bytes 10485760 | tf_op jit(solution)/shard_map/pallas_call | solution.py:328
  55.9 9.7 %all_to_all.16.e_ref = f32[16,8,128]{2,1,0:T(8,128)S(1)} all-to-all(f32[16,8,128]{2,1,0:T(8,128)S(1)} %get-tuple-element.8), channel_id=1, replica_groups=mesh['member'=16,'band_0'=2,'band_1'=4,'band_2'=2] {'band_0','band_1','b..., dimensions={0} | all-to-all | bytes 131072 | tf_op jit(solution)/shard_map/all_to_all | solution.py:292
  65.6 0.0 copy-done.1
  65.6 0.0 copy-done.6
  65.6 0.0 copy-done.7
  65.6 4.8 %shard_map.111 = f32[16,8,48,128]{3,2,1,0:T(8,128)S(1)} custom-call(f32[1024,1024]{1,0:T(8,128)S(1)} %get-tuple-element.7.p_ref, f32[16,8,128]{2,1,0:T(8,128)S(1)} %all_to_all.16.e_ref, f32[64,1024]{1,0:T(8,128)S(1)} %copy-done.1, bf16[4,192,256]{2,1,0:T(8,128)(2,1)S(1)} %copy-done.7, bf16[4,192,256]{2,1,0:T(8,128)(2,1)S(1)} %copy-done.6), custom_call_target="tpu_custom_call" | custom-call | flops 4831838208 | bytes 10485760 | tf_op jit(solution)/shard_map/pallas_call | solution.py:329
  70.4 0.0 copy-start.2
  70.4 0.0 copy-start.3
  70.5 40.7 %all_to_all.17.r_ref = f32[16,8,48,128]{3,2,1,0:T(8,128)S(1)} all-to-all(f32[16,8,48,128]{3,2,1,0:T(8,128)S(1)} %shard_map.111), channel_id=1, replica_groups=mesh['member'=16,'band_0'=2,'band_1'=4,'band_2'=2] {'band_0','band_1','b..., dimensions={0} | all-to-all | bytes 6291456 | tf_op jit(solution)/shard_map/all_to_all | solution.py:292
  111.1 0.0 copy-done.2
  111.1 0.0 copy-done.3
  111.1 4.2 %shard_map.112 = f32[16,48,768]{2,1,0:T(8,128)} custom-call(f32[16,8,48,128]{3,2,1,0:T(8,128)S(1)} %all_to_all.17.r_ref, bf16[2,512,384]{2,1,0:T(8,128)(2,1)S(1)} %copy-done.3, bf16[2,512,384]{2,1,0:T(8,128)(2,1)S(1)} %copy-done.2), custom_call_target="tpu_custom_call" | custom-call | flops 4831838208 | bytes 10485760 | tf_op jit(solution)/shard_map/pallas_call | solution.py:330
Async XLA Ops:
  8.1 44.5 %copy-start = (f32[64,1024]{1,0:T(8,128)S(1)}, f32[64,1024]{1,0:T(8,128)}, u32[]{:S(2)}) copy-start(f32[64,1024]{1,0:T(8,128)} %c_ref.1) | copy-start | bytes 786436
  8.1 44.5 %copy-start.4 = (bf16[4,256,192]{2,1,0:T(8,128)(2,1)S(1)}, bf16[4,256,192]{2,1,0:T(8,128)(2,1)}, u32[]{:S(2)}) copy-start(bf16[4,256,192]{2,1,0:T(8,128)(2,1)} %constant.21.clone.tl_ref) | copy-start | bytes 1179652
  8.1 44.6 %copy-start.5 = (bf16[4,256,192]{2,1,0:T(8,128)(2,1)S(1)}, bf16[4,256,192]{2,1,0:T(8,128)(2,1)}, u32[]{:S(2)}) copy-start(bf16[4,256,192]{2,1,0:T(8,128)(2,1)} %constant.20.clone.th_ref) | copy-start | bytes 1179652
  52.7 12.9 %copy-start.1 = (f32[64,1024]{1,0:T(8,128)S(1)}, f32[64,1024]{1,0:T(8,128)}, u32[]{:S(2)}) copy-start(f32[64,1024]{1,0:T(8,128)} %q_ref.1) | copy-start | bytes 786436
  52.7 12.9 %copy-start.6 = (bf16[4,192,256]{2,1,0:T(8,128)(2,1)S(1)}, bf16[4,192,256]{2,1,0:T(8,128)(2,1)}, u32[]{:S(2)}) copy-start(bf16[4,192,256]{2,1,0:T(8,128)(2,1)} %constant.23.clone.tl_ref) | copy-start | bytes 1179652
  52.7 12.9 %copy-start.7 = (bf16[4,192,256]{2,1,0:T(8,128)(2,1)S(1)}, bf16[4,192,256]{2,1,0:T(8,128)(2,1)}, u32[]{:S(2)}) copy-start(bf16[4,192,256]{2,1,0:T(8,128)(2,1)} %constant.22.clone.th_ref) | copy-start | bytes 1179652
  70.4 40.7 %copy-start.2 = (bf16[2,512,384]{2,1,0:T(8,128)(2,1)S(1)}, bf16[2,512,384]{2,1,0:T(8,128)(2,1)}, u32[]{:S(2)}) copy-start(bf16[2,512,384]{2,1,0:T(8,128)(2,1)} %constant.17.clone.tl_ref) | copy-start | bytes 2359300
  70.4 40.7 %copy-start.3 = (bf16[2,512,384]{2,1,0:T(8,128)(2,1)S(1)}, bf16[2,512,384]{2,1,0:T(8,128)(2,1)}, u32[]{:S(2)}) copy-start(bf16[2,512,384]{2,1,0:T(8,128)(2,1)} %constant.16.clone.th_ref) | copy-start | bytes 2359300
